TPU v7x, 8 devices: a whole 2x2x1 slice. The times are simulated.
8 devices in a mesh: right: 4 (over z, y, x), left: 2 (over core).
Axes of the slice: x: 2, y: 2, z: 1, core: 2. Of those that a mesh axis runs over, the one named last changes fastest.
Arguments:
- psi_init: float32 [768, 2, 2, 768], P('left', None, None, 'right')
- env_left: float32 [768, 20, 768], P('left')
- env_right: float32 [768, 20, 768], P('right')
- mpo_pair: float32 [20, 20, 2, 2, 2, 2], replicated
Outputs:
- output 1: float32 [5], replicated
- output 2: float32 [5], replicated
- output 3: float32 [768, 2, 2, 768], P('left', None, None, 'right')
All inputs are finite; a program needn't handle non-finite values.
Results may differ from a plain program's by a relative error of at most 0.001.
Values sent between devices are 32-bit elements.
A program may use at most 1 GiB of HBM per device.

v0:
```python
import math
import jax
import jax.numpy as jnp
from jax import lax
from jax.sharding import PartitionSpec as P

KRYLOV_STEPS = 5
PREC_MODE = lax.Precision.HIGHEST
BOTH_AXES = ("right", "left")


def project_out(krylov_basis, residual, coeffs):
    for vec_idx, basis_vec in enumerate(krylov_basis):
        residual = residual - coeffs[vec_idx] * basis_vec
    return residual


def global_dots(krylov_basis, residual):
    local_dots = jnp.stack([jnp.sum(basis_vec * residual) for basis_vec in krylov_basis])
    return lax.psum(local_dots, BOTH_AXES)


def solution(mesh):
    n_devices = mesh.shape["left"] * mesh.shape["right"]
    psi_spec = P("left", None, None, "right")

    def local_fn(psi_loc, env_left, env_right, mpo_pair):
        left_full = lax.all_to_all(env_left, "left", 2, 0, tiled=True)

        def apply_ham(in_vec):
            vec_full = lax.all_gather(in_vec, "left", axis=0, tiled=True)
            stage_one = jnp.einsum("alc,asub->lcsub", left_full, vec_full, precision=PREC_MODE, preferred_element_type=jnp.float32)
            stage_two = jnp.einsum("lrsutv,lcsub->rtvcb", mpo_pair, stage_one, precision=PREC_MODE, preferred_element_type=jnp.float32)
            part_out = jnp.einsum("rtvcb,bre->tvce", stage_two, env_right, precision=PREC_MODE, preferred_element_type=jnp.float32)
            reduced = lax.psum_scatter(part_out, "right", scatter_dimension=3, tiled=True)
            return jnp.transpose(reduced, (2, 0, 1, 3))

        init_norm = jnp.sqrt(lax.psum(jnp.sum(psi_loc * psi_loc), BOTH_AXES))
        krylov_basis = [psi_loc / init_norm]
        alpha_list = []
        beta_list = []
        for step_idx in range(KRYLOV_STEPS):
            residual = apply_ham(krylov_basis[-1])
            first_pass = global_dots(krylov_basis, residual)
            alpha_list.append(first_pass[-1])
            residual = project_out(krylov_basis, residual, first_pass)
            second_pass = global_dots(krylov_basis, residual)
            residual = project_out(krylov_basis, residual, second_pass)
            beta_val = jnp.sqrt(lax.psum(jnp.sum(residual * residual), BOTH_AXES))
            beta_list.append(beta_val)
            krylov_basis.append(residual / beta_val)
        out_scale = math.sqrt(float(psi_loc.size * n_devices))
        return jnp.stack(alpha_list), jnp.stack(beta_list), krylov_basis[-1] * out_scale

    lanczos_run = jax.shard_map(
        local_fn,
        mesh=mesh,
        in_specs=(psi_spec, P("left", None, None), P("right", None, None), P()),
        out_specs=(P(), P(), psi_spec),
        check_vma=False,
    )
    return lanczos_run
```

profile of v0, /device:TPU:0, one launch (start us, length us, event | category | flops | bytes accessed | tf_op | source)
XLA Modules:
  0.0 1827.7 jit_solution(10111500755760050649)
XLA Ops:
  9.5 25.3 %psum.112 = f32[]{:T(128)} all-reduce(f32[]{:T(128)} %multiply_reduce_fusion.20), channel_id=1, replica_groups=mesh['right'=4,'left'=2] {'right','left'}, use_global_device_ids=true, to_apply=%region_1.0 | all-reduce | flops 1 | bytes 8 | tf_op jit(solution)/shard_map/psum | solution.py:38
  36.6 26.5 %copy.24 = f32[384,20,768]{0,1,2:T(8,128)} copy(f32[384,20,768]{2,0,1:T(8,128)} %param.5) | data formatting | bytes 47185920 | tf_op args[1]
  96.9 25.8 %copy.26 = f32[2,384,20,384]{3,1,0,2:T(8,128)} copy(f32[2,384,20,384]{1,2,3,0:T(8,128)} %bitcast.4) | data formatting | bytes 47185920 | tf_op jit(solution)/shard_map/all_to_all | solution.py:28
  122.7 61.7 %convolution_bitcast_fusion.4 = f32[20,384,2,2,192,1,1]{1,4,0,3,2,6,5:T(8,128)S(1)} fusion(f32[768,20,384,1,1]{2,0,1,4,3:T(8,128)} %bitcast.297, f32[768,2,2,192]{0,3,2,1:T(8,128)} %all-gather.6.cloned.1.call-done), kind=kOutput, calls=%fused_computation.34 | convolution fusion | flops 54358179840 | bytes 49545216 | tf_op jit(solution)/shard_map/alc,asub->lcsub/dot_general | solution.py:32
  184.3 56.3 %fusion.20 = f32[20,2,2,384,192]{3,0,2,1,4:T(8,128)} fusion(f32[20,384,2,2,192,1,1]{1,4,0,3,2,6,5:T(8,128)S(1)} %convolution_bitcast_fusion.4, f32[20,20,2,2,2,2]{0,1,3,2,5,4:T(8,128)S(1)} %copy.28), kind=kOutput, calls=%fused_computation.20 | convolution fusion | flops 5662310400 | bytes 47211520 | tf_op jit(solution)/shard_map/lrsutv,lcsub->rtvcb/dot_general | solution.py:33
  240.6 70.5 %fusion.45 = f32[2,2,384,768]{2,3,1,0:T(8,128)} fusion(f32[192,20,768]{2,0,1:T(8,128)} %param.6, f32[20,2,2,384,192]{3,0,2,1,4:T(8,128)} %fusion.20), kind=kOutput, calls=%fused_computation.40 | convolution fusion | flops 54358179840 | bytes 40108032 | tf_op jit(solution)/shard_map/rtvcb,bre->tvce/dot_general | solution.py:34
  311.3 52.3 %reduce-scatter.6.cloned.1.call-done = f32[2,2,384,192]{2,3,1,0:T(8,128)} async-done(((f32[2,2,384,768]{2,3,1,0:T(8,128)}), f32[2,2,384,192]{2,3,1,0:T(8,128)}) %reduce-scatter.6.cloned.1.call-update) | async-done | bytes 1179664 | tf_op jit(solution)/shard_map/reduce_scatter | solution.py:35
  390.0 24.4 %psum.114 = f32[]{:T(128)} all-reduce(f32[]{:T(128)} %multiply_reduce_fusion.19), channel_id=1, replica_groups=mesh['right'=4,'left'=2] {'right','left'}, use_global_device_ids=true, to_apply=%region_6.0 | all-reduce | flops 1 | bytes 8 | tf_op jit(solution)/shard_map/psum | solution.py:20
  416.6 23.4 %psum.115 = f32[]{:T(128)} all-reduce(f32[]{:T(128)} %multiply_reduce_fusion.18), channel_id=1, replica_groups=mesh['right'=4,'left'=2] {'right','left'}, use_global_device_ids=true, to_apply=%region_8.0 | all-reduce | flops 1 | bytes 8 | tf_op jit(solution)/shard_map/psum | solution.py:49
  453.6 61.7 %convolution_bitcast_fusion.3 = f32[20,384,2,2,192,1,1]{1,4,0,3,2,6,5:T(8,128)S(1)} fusion(f32[768,20,384,1,1]{2,0,1,4,3:T(8,128)} %bitcast.298, f32[768,2,2,192]{0,3,2,1:T(8,128)} %all-gather.8.cloned.1.call-done), kind=kOutput, calls=%fused_computation.33 | convolution fusion | flops 54358179840 | bytes 49545216 | tf_op jit(solution)/shard_map/alc,asub->lcsub/dot_general | solution.py:32
  515.3 56.2 %fusion.23 = f32[20,2,2,384,192]{3,0,2,1,4:T(8,128)} fusion(f32[20,384,2,2,192,1,1]{1,4,0,3,2,6,5:T(8,128)S(1)} %convolution_bitcast_fusion.3, f32[20,20,2,2,2,2]{0,1,3,2,5,4:T(8,128)S(1)} %copy.28), kind=kOutput, calls=%fused_computation.21 | convolution fusion | flops 5662310400 | bytes 47211520 | tf_op jit(solution)/shard_map/lrsutv,lcsub->rtvcb/dot_general | solution.py:33
  571.5 70.5 %fusion.50 = f32[2,2,384,768]{2,3,1,0:T(8,128)} fusion(f32[192,20,768]{2,0,1:T(8,128)} %param.6, f32[20,2,2,384,192]{3,0,2,1,4:T(8,128)} %fusion.23), kind=kOutput, calls=%fused_computation.41 | convolution fusion | flops 54358179840 | bytes 40108032 | tf_op jit(solution)/shard_map/rtvcb,bre->tvce/dot_general | solution.py:34
  642.1 52.5 %reduce-scatter.8.cloned.1.call-done = f32[2,2,384,192]{2,3,1,0:T(8,128)} async-done(((f32[2,2,384,768]{2,3,1,0:T(8,128)}), f32[2,2,384,192]{2,3,1,0:T(8,128)}) %reduce-scatter.8.cloned.1.call-update) | async-done | bytes 1179664 | tf_op jit(solution)/shard_map/reduce_scatter | solution.py:35
  725.1 23.9 %psum.117 = f32[2]{0:T(128)S(1)} all-reduce(f32[2]{0:T(128)S(1)} %pad_maximum_fusion.1), channel_id=1, replica_groups=mesh['right'=4,'left'=2] {'right','left'}, use_global_device_ids=true, to_apply=%region_15.0 | all-reduce | flops 2 | bytes 16 | tf_op jit(solution)/shard_map/psum | solution.py:20
  754.5 23.3 %psum.118 = f32[]{:T(128)} all-reduce(f32[]{:T(128)} %get-tuple-element.40), channel_id=1, replica_groups=mesh['right'=4,'left'=2] {'right','left'}, use_global_device_ids=true, to_apply=%region_17.0 | all-reduce | flops 1 | bytes 8 | tf_op jit(solution)/shard_map/psum | solution.py:49
  789.9 61.7 %convolution_bitcast_fusion.2 = f32[20,384,2,2,192,1,1]{1,4,0,3,2,6,5:T(8,128)S(1)} fusion(f32[768,20,384,1,1]{2,0,1,4,3:T(8,128)} %bitcast.299, f32[768,2,2,192]{0,3,2,1:T(8,128)} %all-gather.10.cloned.1.call-done), kind=kOutput, calls=%fused_computation.32 | convolution fusion | flops 54358179840 | bytes 49545216 | tf_op jit(solution)/shard_map/alc,asub->lcsub/dot_general | solution.py:32
  851.6 56.2 %fusion.26 = f32[20,2,2,384,192]{3,0,2,1,4:T(8,128)} fusion(f32[20,384,2,2,192,1,1]{1,4,0,3,2,6,5:T(8,128)S(1)} %convolution_bitcast_fusion.2, f32[20,20,2,2,2,2]{0,1,3,2,5,4:T(8,128)S(1)} %copy-done.5), kind=kOutput, calls=%fused_computation.22 | convolution fusion | flops 5662310400 | bytes 47211520 | tf_op jit(solution)/shard_map/lrsutv,lcsub->rtvcb/dot_general | solution.py:33
  907.8 70.5 %fusion.55 = f32[2,2,384,768]{2,3,1,0:T(8,128)} fusion(f32[192,20,768]{2,0,1:T(8,128)} %param.6, f32[20,2,2,384,192]{3,0,2,1,4:T(8,128)} %fusion.26), kind=kOutput, calls=%fused_computation.42 | convolution fusion | flops 54358179840 | bytes 40108032 | tf_op jit(solution)/shard_map/rtvcb,bre->tvce/dot_general | solution.py:34
  978.4 52.5 %reduce-scatter.10.cloned.1.call-done = f32[2,2,384,192]{2,3,1,0:T(8,128)} async-done(((f32[2,2,384,768]{2,3,1,0:T(8,128)}), f32[2,2,384,192]{2,3,1,0:T(8,128)}) %reduce-scatter.10.cloned.1.call-update) | async-done | bytes 1179664 | tf_op jit(solution)/shard_map/reduce_scatter | solution.py:35
  1065.4 23.9 %psum.120 = f32[3]{0:T(128)S(1)} all-reduce(f32[3]{0:T(128)S(1)} %pad_maximum_fusion.3), channel_id=1, replica_groups=mesh['right'=4,'left'=2] {'right','left'}, use_global_device_ids=true, to_apply=%region_26.0 | all-reduce | flops 3 | bytes 24 | tf_op jit(solution)/shard_map/psum | solution.py:20
  1131.7 61.7 %convolution_bitcast_fusion.1 = f32[20,384,2,2,192,1,1]{1,4,0,3,2,6,5:T(8,128)S(1)} fusion(f32[768,20,384,1,1]{2,0,1,4,3:T(8,128)} %bitcast.300, f32[768,2,2,192]{0,3,2,1:T(8,128)} %all-gather.12.cloned.1.call-done), kind=kOutput, calls=%fused_computation.31 | convolution fusion | flops 54358179840 | bytes 49545216 | tf_op jit(solution)/shard_map/alc,asub->lcsub/dot_general | solution.py:32
  1193.4 56.2 %fusion.29 = f32[20,2,2,384,192]{3,0,2,1,4:T(8,128)} fusion(f32[20,384,2,2,192,1,1]{1,4,0,3,2,6,5:T(8,128)S(1)} %convolution_bitcast_fusion.1, f32[20,20,2,2,2,2]{0,1,3,2,5,4:T(8,128)S(1)} %copy-done.6), kind=kOutput, calls=%fused_computation.23 | convolution fusion | flops 5662310400 | bytes 47211520 | tf_op jit(solution)/shard_map/lrsutv,lcsub->rtvcb/dot_general | solution.py:33
  1249.6 70.5 %fusion.60 = f32[2,2,384,768]{2,3,1,0:T(8,128)} fusion(f32[192,20,768]{2,0,1:T(8,128)} %param.6, f32[20,2,2,384,192]{3,0,2,1,4:T(8,128)} %fusion.29), kind=kOutput, calls=%fused_computation.43 | convolution fusion | flops 54358179840 | bytes 40108032 | tf_op jit(solution)/shard_map/rtvcb,bre->tvce/dot_general | solution.py:34
  1320.7 52.1 %reduce-scatter.12.cloned.1.call-done = f32[2,2,384,192]{2,3,1,0:T(8,128)} async-done(((f32[2,2,384,768]{2,3,1,0:T(8,128)}), f32[2,2,384,192]{2,3,1,0:T(8,128)}) %reduce-scatter.12.cloned.1.call-update) | async-done | bytes 1179664 | tf_op jit(solution)/shard_map/reduce_scatter | solution.py:35
  1409.6 23.9 %psum.123 = f32[4]{0:T(128)S(1)} all-reduce(f32[4]{0:T(128)S(1)} %pad_maximum_fusion.5), channel_id=1, replica_groups=mesh['right'=4,'left'=2] {'right','left'}, use_global_device_ids=true, to_apply=%region_39.0 | all-reduce | flops 4 | bytes 32 | tf_op jit(solution)/shard_map/psum | solution.py:20
  1440.5 23.3 %psum.124 = f32[]{:T(128)} all-reduce(f32[]{:T(128)} %get-tuple-element.34), channel_id=1, replica_groups=mesh['right'=4,'left'=2] {'right','left'}, use_global_device_ids=true, to_apply=%region_41.0 | all-reduce | flops 1 | bytes 8 | tf_op jit(solution)/shard_map/psum | solution.py:49
  1477.2 61.7 %convolution_bitcast_fusion = f32[20,384,2,2,192,1,1]{1,4,0,3,2,6,5:T(8,128)S(1)} fusion(f32[768,20,384,1,1]{2,0,1,4,3:T(8,128)} %bitcast.301, f32[768,2,2,192]{0,3,2,1:T(8,128)} %all-gather.14.cloned.1.call-done), kind=kOutput, calls=%fused_computation.30 | convolution fusion | flops 54358179840 | bytes 49545216 | tf_op jit(solution)/shard_map/alc,asub->lcsub/dot_general | solution.py:32
  1538.9 56.0 %fusion.32 = f32[20,2,2,384,192]{3,0,2,1,4:T(8,128)} fusion(f32[20,384,2,2,192,1,1]{1,4,0,3,2,6,5:T(8,128)S(1)} %convolution_bitcast_fusion, f32[20,20,2,2,2,2]{0,1,3,2,5,4:T(8,128)S(1)} %copy-done.7), kind=kOutput, calls=%fused_computation.24 | convolution fusion | flops 5662310400 | bytes 47211520 | tf_op jit(solution)/shard_map/lrsutv,lcsub->rtvcb/dot_general | solution.py:33
  1594.9 70.8 %fusion.65 = f32[2,2,384,768]{2,3,1,0:T(8,128)} fusion(f32[192,20,768]{2,0,1:T(8,128)} %param.6, f32[20,2,2,384,192]{3,0,2,1,4:T(8,128)} %fusion.32), kind=kOutput, calls=%fused_computation.44 | convolution fusion | flops 54358179840 | bytes 40108032 | tf_op jit(solution)/shard_map/rtvcb,bre->tvce/dot_general | solution.py:34
  1665.7 52.5 %reduce-scatter.14.cloned.1.call-done = f32[2,2,384,192]{2,3,1,0:T(8,128)} async-done(((f32[2,2,384,768]{2,3,1,0:T(8,128)}), f32[2,2,384,192]{2,3,1,0:T(8,128)}) %reduce-scatter.14.cloned.1.call-update) | async-done | bytes 1179664 | tf_op jit(solution)/shard_map/reduce_scatter | solution.py:35
  1762.0 23.9 %psum.126 = f32[5]{0:T(128)S(1)} all-reduce(f32[5]{0:T(128)S(1)} %stack.177), channel_id=1, replica_groups=mesh['right'=4,'left'=2] {'right','left'}, use_global_device_ids=true, to_apply=%region_54.0 | all-reduce | flops 5 | bytes 40 | tf_op jit(solution)/shard_map/psum | solution.py:20
  1793.7 23.2 %psum.127 = f32[]{:T(128)} all-reduce(f32[]{:T(128)} %get-tuple-element.31), channel_id=1, replica_groups=mesh['right'=4,'left'=2] {'right','left'}, use_global_device_ids=true, to_apply=%region_56.0 | all-reduce | flops 1 | bytes 8 | tf_op jit(solution)/shard_map/psum | solution.py:49
  (92 shorter events, 314.0 us)
Async XLA Ops:
  7.2 28.3 %copy-start = (f32[384,2,2,192]{0,3,2,1:T(8,128)S(1)}, f32[384,2,2,192]{0,3,2,1:T(8,128)}, u32[]{:S(2)}) copy-start(f32[384,2,2,192]{0,3,2,1:T(8,128)} %param.4) | copy-start | bytes 3538948
  7.2 115.5 %all-gather.6.cloned.1.call-start = ((), (), s32[]{:S(2)}) async-start(), calls=%async_computation.6 | async-start | bytes 3538944 | tf_op jit(solution)/shard_map/all_gather | solution.py:31
  63.1 12.7 copy-start.8
  63.1 33.8 %all-to-all-start = ((f32[384,20,768]{0,1,2:T(8,128)}), f32[384,20,768]{0,1,2:T(8,128)}, u32[]{:S(2)}, u32[]{:S(2)}) async-start(f32[384,20,768]{0,1,2:T(8,128)} %copy.24), calls=%async_computation | async-start | bytes 56623104 | tf_op jit(solution)/shard_map/all_to_all | solution.py:28
  75.6 288.0 %reduce-scatter.6.cloned.1.call-start = ((), (), s32[]{:S(2)}) async-start(), calls=%async_computation.7 | async-start | bytes 5898240 | tf_op jit(solution)/shard_map/reduce_scatter | solution.py:35
  76.0 439.3 %copy-start.4 = (f32[20,20,2,2,2,2]{0,1,3,2,5,4:T(8,128)}, f32[20,20,2,2,2,2]{0,1,3,2,5,4:T(8,128)S(1)}, u32[]{:S(2)}) copy-start(f32[20,20,2,2,2,2]{0,1,3,2,5,4:T(8,128)S(1)} %copy.28) | copy-start | bytes 76804
  311.2 142.4 %all-gather.8.cloned.1.call-start = ((), (), s32[]{:S(2)}) async-start(), calls=%async_computation.8 | async-start | bytes 3538944 | tf_op jit(solution)/shard_map/all_gather | solution.py:31
  363.6 24.9 %copy-start.2 = (f32[2,2,384,192]{2,3,1,0:T(8,128)S(1)}, f32[2,2,384,192]{2,3,1,0:T(8,128)}, u32[]{:S(2)}) copy-start(f32[2,2,384,192]{2,3,1,0:T(8,128)} %reduce-scatter.6.cloned.1.call-done) | copy-start | bytes 3538948
  443.3 251.3 %reduce-scatter.8.cloned.1.call-start = ((), (), s32[]{:S(2)}) async-start(), calls=%async_computation.9 | async-start | bytes 5898240 | tf_op jit(solution)/shard_map/reduce_scatter | solution.py:35
  642.0 52.6 %copy-start.1 = (f32[384,2,2,192]{0,3,2,1:T(8,128)S(1)}, f32[384,2,2,192]{0,3,2,1:T(8,128)}, u32[]{:S(2)}) copy-start(f32[384,2,2,192]{0,3,2,1:T(8,128)} %broadcast_divide_fusion.3) | copy-start | bytes 3538948
  642.1 147.8 %all-gather.10.cloned.1.call-start = ((), (), s32[]{:S(2)}) async-start(), calls=%async_computation.10 | async-start | bytes 3538944 | tf_op jit(solution)/shard_map/all_gather | solution.py:31
  694.6 26.8 %copy-start.3 = (f32[2,2,384,192]{2,3,1,0:T(8,128)S(1)}, f32[2,2,384,192]{2,3,1,0:T(8,128)}, u32[]{:S(2)}) copy-start(f32[2,2,384,192]{2,3,1,0:T(8,128)} %reduce-scatter.8.cloned.1.call-done) | copy-start | bytes 3538948
  779.5 251.3 %reduce-scatter.10.cloned.1.call-start = ((), (), s32[]{:S(2)}) async-start(), calls=%async_computation.11 | async-start | bytes 5898240 | tf_op jit(solution)/shard_map/reduce_scatter | solution.py:35
  789.9 61.7 %copy-start.5 = (f32[20,20,2,2,2,2]{0,1,3,2,5,4:T(8,128)S(1)}, f32[20,20,2,2,2,2]{0,1,3,2,5,4:T(8,128)}, u32[]{:S(2)}) copy-start(f32[20,20,2,2,2,2]{0,1,3,2,5,4:T(8,128)} %copy-done.4) | copy-start | bytes 76804
  978.3 153.4 %all-gather.12.cloned.1.call-start = ((), (), s32[]{:S(2)}) async-start(), calls=%async_computation.12 | async-start | bytes 3538944 | tf_op jit(solution)/shard_map/all_gather | solution.py:31
  1121.4 251.3 %reduce-scatter.12.cloned.1.call-start = ((), (), s32[]{:S(2)}) async-start(), calls=%async_computation.13 | async-start | bytes 5898240 | tf_op jit(solution)/shard_map/reduce_scatter | solution.py:35
  1131.7 61.7 %copy-start.6 = (f32[20,20,2,2,2,2]{0,1,3,2,5,4:T(8,128)S(1)}, f32[20,20,2,2,2,2]{0,1,3,2,5,4:T(8,128)}, u32[]{:S(2)}) copy-start(f32[20,20,2,2,2,2]{0,1,3,2,5,4:T(8,128)} %copy-done.4) | copy-start | bytes 76804
  1320.2 157.0 %all-gather.14.cloned.1.call-start = ((), (), s32[]{:S(2)}) async-start(), calls=%async_computation.14 | async-start | bytes 3538944 | tf_op jit(solution)/shard_map/all_gather | solution.py:31
  1466.8 251.4 %reduce-scatter.14.cloned.1.call-start = ((), (), s32[]{:S(2)}) async-start(), calls=%async_computation.15 | async-start | bytes 5898240 | tf_op jit(solution)/shard_map/reduce_scatter | solution.py:35
  1477.2 61.7 %copy-start.7 = (f32[20,20,2,2,2,2]{0,1,3,2,5,4:T(8,128)S(1)}, f32[20,20,2,2,2,2]{0,1,3,2,5,4:T(8,128)}, u32[]{:S(2)}) copy-start(f32[20,20,2,2,2,2]{0,1,3,2,5,4:T(8,128)} %copy-done.4) | copy-start | bytes 76804
Sparse Core Ops, SparseCore 0:
  36.7 9.2 all-gather.5
  311.3 52.1 reduce-scatter.5
  443.4 10.1 all-gather.7
  642.2 52.3 reduce-scatter.7
  779.7 10.1 all-gather.9
  978.5 52.3 reduce-scatter.9
  1121.5 10.1 all-gather.11
  1320.3 52.3 reduce-scatter.11
  1467.0 10.1 all-gather.13
  1665.8 52.3 reduce-scatter.13
where the time goes:
time: 1830 us
  matrix products  942 us (51%)
  blocking collectives  374 us (20%)
  waiting for transfers between devices  324 us (18%)
  other arithmetic  87.5 us (5%)
  local copies, waits for them, and re-layouts  68.1 us (4%)
  between operations  18.8 us (1%)
    dot_general x5, matrix products, apply_ham(): jnp.einsum('rtvcb,bre->tvce', stage_two, env_right, precision=PREC_MODE,...  353 us
    dot_general x5, matrix products, apply_ham(): jnp.einsum('alc,asub->lcsub', left_full, vec_full, precision=PREC_MODE, p...  308 us
    dot_general x5, matrix products, apply_ham(): jnp.einsum('lrsutv,lcsub->rtvcb', mpo_pair, stage_one, precision=PREC_MOD...  281 us
    reduce_scatter x5, waiting for transfers between devices, apply_ham(): lax.psum_scatter(part_out, 'right', scatter_dimension=3, tiled=True)  262 us
    psum x10, blocking collectives, global_dots(): return lax.psum(local_dots, BOTH_AXES)  232 us
    psum x5, blocking collectives, local_fn(): beta_val = jnp.sqrt(lax.psum(jnp.sum(residual * residual), BOTH_AXES))  116 us
    all_gather x5, waiting for transfers between devices, apply_ham(): vec_full = lax.all_gather(in_vec, 'left', axis=0, tiled=True)  41.1 us
  transfers between devices with their start and end apart: 11, of which 10 were waited for; matrix products, arithmetic and copies ran while one was open for 3% of the time, Pallas kernels for 0%

commit v1 on v0

v1 whole, which is shorter than its diff:
```python
import math
import jax
import jax.numpy as jnp
from jax import lax
from jax.experimental import pallas as pl
from jax.experimental.pallas import tpu as pltpu
from jax.sharding import PartitionSpec as P

F32, BF16 = jnp.float32, jnp.bfloat16
MESH = pl.DeviceIdType.MESH
KRYLOV_STEPS = 5
N_RIGHT, N_LEFT = 4, 2
N_DEV = N_RIGHT * N_LEFT
BOND = 768
MPO = 20
ROWS = BOND // N_LEFT
COLS = BOND // N_RIGHT
LB = 64
NBLK = ROWS // LB
HALF = LB // 2
CS, CX = LB + 8, HALF + 8
UNITS = 16
K_FIRST, K_SECOND, K_NORM = 0, 1, 2


def split3(x):
    hi = x.astype(BF16)
    rest = x - hi.astype(F32)
    mid = rest.astype(BF16)
    low = (rest - mid.astype(F32)).astype(BF16)
    return hi, mid, low


def dot(a, b):
    return jnp.dot(a, b, preferred_element_type=F32)


def dot6(a, b):
    return (dot(a[0], b[0]) + (dot(a[0], b[1]) + dot(a[1], b[0]))
            + (dot(a[0], b[2]) + dot(a[1], b[1]) + dot(a[2], b[0])))


def lane_pair(x0, x1):
    left = lax.broadcasted_iota(jnp.int32, x0.shape, 1) < 64
    return (jnp.where(left, x0, pltpu.roll(x1, 64, 1)),
            jnp.where(left, pltpu.roll(x0, 64, 1), x1))


def kernel(psi, l_hi, l_mid, l_low, r_hi, r_mid, r_low, w_main, w_extra,
           out_small, out_psi,
           lb, rm, rx, vs, t1m, t1x, zm, zx, zs, yb, sb, rv, basis, u, ab, coef, scal,
           l_sem, r_sem, io_sem, rs_send, rs_recv, pu_send, pu_recv, ar_send, ar_recv):
    my_r, my_l = lax.axis_index("right"), lax.axis_index("left")
    me = my_r * N_LEFT + my_l
    own0 = pl.multiple_of(my_l * ROWS, ROWS)
    oth0 = pl.multiple_of((1 - my_l) * ROWS, ROWS)
    partner = (my_r, 1 - my_l)
    odd = lax.rem(my_r, 2)
    main0 = pl.multiple_of(odd * 64, 64)
    extra0 = pl.multiple_of((1 - odd) * 128, 64)
    l_hbm = (l_hi, l_mid, l_low)
    r_hbm = (r_hi, r_mid, r_low)

    def l_copies(blk):
        row = pl.multiple_of(blk * LB, LB)
        return [pltpu.make_async_copy(l_hbm[i].at[:, pl.ds(row, LB), :], lb.at[i], l_sem.at[i])
                for i in range(3)]

    def r_copies():
        return ([pltpu.make_async_copy(r_hbm[i].at[:, pl.ds(main0, 128), :], rm.at[i], r_sem.at[i])
                 for i in range(3)]
                + [pltpu.make_async_copy(r_hbm[i].at[:, pl.ds(extra0, 64), :], rx.at[i], r_sem.at[3 + i])
                   for i in range(3)])

    def piece_copies(blk):
        slot = lax.rem(blk, 2)
        row = pl.multiple_of(blk * LB, LB)
        out = []
        for p in range(1, N_RIGHT):
            to = lax.rem(my_r + p, N_RIGHT)
            out.append(pltpu.make_async_remote_copy(
                src_ref=sb.at[slot, to], dst_ref=rv.at[p - 1, pl.ds(row, LB), :],
                send_sem=rs_send.at[p - 1, slot], recv_sem=rs_recv.at[p - 1, blk],
                device_id=(to, my_l), device_id_type=MESH))
        return out

    def partner_copy(blk):
        row = pl.multiple_of(own0 + blk * LB, LB)
        return pltpu.make_async_remote_copy(
            src_ref=u.at[pl.ds(row, LB), :], dst_ref=u.at[pl.ds(row, LB), :],
            send_sem=pu_send.at[blk], recv_sem=pu_recv.at[blk],
            device_id=partner, device_id_type=MESH)

    def sum_copies(kind):
        out = []
        for p in range(1, N_DEV):
            to = lax.rem(me + p, N_DEV)
            out.append(pltpu.make_async_remote_copy(
                src_ref=ab.at[kind, me], dst_ref=ab.at[kind, me],
                send_sem=ar_send.at[kind, p - 1], recv_sem=ar_recv.at[kind, p - 1],
                device_id=(to // N_LEFT, lax.rem(to, N_LEFT)), device_id_type=MESH))
        return out

    def sum_start(kind):
        for copy in sum_copies(kind):
            copy.start()

    def sum_finish(kind):
        for copy in sum_copies(kind):
            copy.wait()
        total = ab[kind, 0]
        for d in range(1, N_DEV):
            total = total + ab[kind, d]
        return jnp.broadcast_to(jnp.sum(total, axis=1, keepdims=True), (8, BOND))

    def put_row(kind, i, acc):
        rows = jnp.sum(acc, axis=0, keepdims=True)
        part = rows[:, 0:128]
        for n in range(1, acc.shape[1] // 128):
            part = part + rows[:, n * 128:(n + 1) * 128]
        ab[kind, me, pl.ds(i, 1), :] = part

    for copy in l_copies(0):
        copy.start()
    for copy in r_copies():
        copy.start()
    psi_in = pltpu.make_async_copy(psi, u.at[pl.ds(own0, ROWS), :], io_sem)
    psi_in.start()
    for kind in range(3):
        ab[kind, me] = jnp.zeros((8, 128), F32)
    coef[...] = jnp.zeros_like(coef)
    scal[...] = jnp.zeros_like(scal)
    out_small[...] = jnp.zeros_like(out_small)

    def clear(i, _):
        row = pl.multiple_of(i * 8, 8)
        for n in range(1, KRYLOV_STEPS):
            basis[n, pl.ds(row, 8), :] = jnp.zeros((8, BOND), F32)
        return 0
    lax.fori_loop(0, BOND // 8, clear, 0)

    barrier = pltpu.get_barrier_semaphore()
    for p in range(1, N_DEV):
        to = lax.rem(me + p, N_DEV)
        pl.semaphore_signal(barrier, inc=1, device_id=(to // N_LEFT, lax.rem(to, N_LEFT)),
                            device_id_type=MESH)
    pl.semaphore_wait(barrier, N_DEV - 1)

    def finalize(dst):
        def rows(base, with_norm):
            def body(i, acc):
                row = pl.multiple_of(base + i * 16, 16)
                out = []
                for n in range(2):
                    cols = pl.ds(n * 384, 384)
                    x = u[pl.ds(row, 16), cols]
                    for m in range(KRYLOV_STEPS):
                        x = x - coef[1, pl.ds(m, 1), cols] * basis[m, pl.ds(row, 16), cols]
                    x = x * scal[pl.ds(0, 1), cols]
                    basis[dst, pl.ds(row, 16), cols] = x
                    for t, part in enumerate(split3(x)):
                        vs[t, pl.ds(row, 16), cols] = part
                    if with_norm:
                        x2 = x * x
                        out.append(acc[n] + (x2[:8] + x2[8:]))
                return tuple(out) if with_norm else 0
            init = (jnp.zeros((8, 384), F32),) * 2 if with_norm else 0
            return lax.fori_loop(0, ROWS // 16, body, init)
        acc = rows(own0, True)
        put_row(K_NORM, 0, acc[0] + acc[1])
        rows(oth0, False)
        sum_start(K_NORM)

    def norm_scale():
        root = jnp.sqrt(scal[pl.ds(2, 1), :])
        scal[pl.ds(1, 1), :] = root
        scal[pl.ds(0, 1), :] = 1.0 / root

    psi_in.wait()

    def greet(blk, _):
        partner_copy(blk).start()
        return 0
    lax.fori_loop(0, NBLK, greet, 0)

    def square(i, acc):
        x = u[pl.ds(pl.multiple_of(own0 + i * 8, 8), 8), :]
        return acc + x * x
    put_row(K_SECOND, 5, lax.fori_loop(0, ROWS // 8, square, jnp.zeros((8, BOND), F32)))
    sum_start(K_SECOND)

    def partner_wait(blk, _):
        partner_copy(blk).wait()
        return 0
    lax.fori_loop(0, NBLK, partner_wait, 0)
    scal[pl.ds(2, 1), :] = sum_finish(K_SECOND)[5:6, :]
    norm_scale()
    finalize(0)

    def stage_one(i, _):
        l0 = i * 4
        a = [lb[t, pl.ds(l0, 4)].reshape(4 * LB, BOND) for t in range(3)]
        for n in range(3):
            t1 = dot6(a, [vs[t, :, n * 256:(n + 1) * 256] for t in range(3)])
            for h in range(2):
                t1h = t1[:, h * 128:(h + 1) * 128]
                for d in range(4):
                    x = t1h[d * LB:(d + 1) * LB]
                    if n < 2:
                        row = pl.multiple_of(((2 * n + h) * MPO + l0 + d) * CS, 8)
                        t1m[pl.ds(row, LB), :] = x
                    else:
                        row = pl.multiple_of((h * MPO + l0 + d) * 2 * CX, 8)
                        x0, x1 = lane_pair(x[:HALF], x[HALF:])
                        t1x[pl.ds(row, HALF), :] = x0
                        t1x[pl.ds(row + CX, HALF), :] = x1
        return 0

    def mpo_units(src, dst, w_ref, stride):
        def body(i, _):
            for n in range(UNITS):
                c = (i * UNITS + n) * 2
                x = jnp.concatenate([src[pl.ds(c, 80, stride=stride), :],
                                     src[pl.ds(c + 1, 80, stride=stride), :]], axis=1)
                t2 = dot(w_ref[...], jnp.concatenate(split3(x), axis=0))
                t2 = t2[0:80] + (t2[80:160] + t2[160:240])
                dst[pl.ds(c, 80, stride=stride), :] = t2[:, :128]
                dst[pl.ds(c + 1, 80, stride=stride), :] = t2[:, 128:]
            return 0
        return body

    def gather_main(r, _):
        cols = pl.ds(pl.multiple_of(r * 128, 128), 128)
        for t in range(4):
            x = zm[pl.ds(pl.multiple_of((r * 4 + t) * CS, 8), LB), :]
            for i, part in enumerate(split3(x)):
                zs[i, t * LB:(t + 1) * LB, cols] = part
        return 0

    def gather_extra(q, _):
        cols = pl.ds(pl.multiple_of(MPO * 128 + q * 128, 128), 128)
        for t in range(4):
            x0 = zx[pl.ds(pl.multiple_of((q * 8 + t) * CX, 8), HALF), :]
            x1 = zx[pl.ds(pl.multiple_of((q * 8 + 4 + t) * CX, 8), HALF), :]
            x = jnp.concatenate(lane_pair(x0, x1), axis=0)
            for i, part in enumerate(split3(x)):
                zs[i, t * LB:(t + 1) * LB, cols] = part
        return 0

    def stage_three(n, _):
        cols = pl.ds(pl.multiple_of(n * 256, 256), 256)
        b = [jnp.concatenate([rm[t, :, :, cols].reshape(MPO * 128, 256),
                              rx[t, :, :, cols].reshape(MPO * 64, 256)], axis=0) for t in range(3)]
        yb[:, cols] = dot6([zs[t] for t in range(3)], b)
        return 0

    def pack(blk):
        slot = lax.rem(blk, 2)
        for to in range(N_RIGHT):
            lane = (0, 2, 3, 5)[to] * 128
            for t in range(4):
                sb[slot, to, :, t * 128:(t + 1) * 128] = yb[t * LB:(t + 1) * LB, lane:lane + 128]
        for pair in range(2):
            lane = (1, 4)[pair] * 128
            for h in range(2):
                y0 = yb[(2 * h) * LB:(2 * h + 1) * LB, lane:lane + 128]
                y1 = yb[(2 * h + 1) * LB:(2 * h + 2) * LB, lane:lane + 128]
                for k, x in enumerate(lane_pair(y0, y1)):
                    sb[slot, 2 * pair + k, :, 512 + h * 128:640 + h * 128] = x

    def reduce(blk):
        slot = lax.rem(blk, 2)
        for copy in piece_copies(blk):
            copy.wait()
        row = pl.multiple_of(blk * LB, LB)
        x = (sb[slot, my_r] + rv[0, pl.ds(row, LB), :]) + (rv[1, pl.ds(row, LB), :] + rv[2, pl.ds(row, LB), :])
        u[pl.ds(pl.multiple_of(own0 + row, LB), LB), :] = x * scal[pl.ds(3, 1), :]
        partner_copy(blk).start()

    def finish_norm(step):
        total = sum_finish(K_NORM)[0:1, :]
        root = jnp.sqrt(total)
        scal[pl.ds(3, 1), :] = 1.0 / root
        out_small[pl.ds(8 + step, 1), :] = (scal[pl.ds(1, 1), :] * root)[:, :128]

    def krylov_step(step, _):
        def block(blk, _):
            for copy in l_copies(blk):
                copy.wait()
            lax.fori_loop(0, MPO // 4, stage_one, 0)
            for copy in l_copies(lax.rem(blk + 1, NBLK)):
                copy.start()
            lax.fori_loop(0, LB // 2 // UNITS, mpo_units(t1m, zm, w_main, CS), 0)
            lax.fori_loop(0, HALF // 2 // UNITS, mpo_units(t1x, zx, w_extra, CX), 0)
            lax.fori_loop(0, MPO, gather_main, 0)
            lax.fori_loop(0, MPO // 2, gather_extra, 0)

            @pl.when((step == 0) & (blk == 0))
            def _():
                for copy in r_copies():
                    copy.wait()

            lax.fori_loop(0, 3, stage_three, 0)
            pack(blk)
            for copy in piece_copies(blk):
                copy.start()

            @pl.when(blk == 0)
            def _():
                finish_norm(step)

                def rescale(i, _):
                    row = pl.multiple_of(i * 16, 16)
                    basis[step, pl.ds(row, 16), :] = basis[step, pl.ds(row, 16), :] * scal[pl.ds(3, 1), :]
                    return 0
                lax.fori_loop(0, BOND // 16, rescale, 0)

            @pl.when(blk > 0)
            def _():
                reduce(blk - 1)
            return 0

        lax.fori_loop(0, NBLK, block, 0)
        reduce(jnp.int32(NBLK - 1))

        def first(i, acc):
            row = pl.multiple_of(own0 + i * 8, 8)
            x = u[pl.ds(row, 8), :]
            return tuple(acc[m] + x * basis[m, pl.ds(row, 8), :] for m in range(KRYLOV_STEPS))
        acc = lax.fori_loop(0, ROWS // 8, first, (jnp.zeros((8, BOND), F32),) * KRYLOV_STEPS)
        for m in range(KRYLOV_STEPS):
            put_row(K_FIRST, m, acc[m])
        sum_start(K_FIRST)
        coef[0] = sum_finish(K_FIRST)
        mine = lax.broadcasted_iota(jnp.int32, (8, 128), 0) == step
        out_small[pl.ds(step, 1), :] = jnp.sum(jnp.where(mine, coef[0, :, 0:128], 0.0), axis=0, keepdims=True)

        def project(base, with_dots):
            def body(i, acc):
                row = pl.multiple_of(base + i * 8, 8)
                new = []
                for n in range(2):
                    cols = pl.ds(n * 384, 384)
                    x = u[pl.ds(row, 8), cols]
                    vecs = [basis[m, pl.ds(row, 8), cols] for m in range(KRYLOV_STEPS)]
                    for m in range(KRYLOV_STEPS):
                        x = x - coef[0, pl.ds(m, 1), cols] * vecs[m]
                    u[pl.ds(row, 8), cols] = x
                    if with_dots:
                        prods = [x * vec for vec in vecs] + [x * x]
                        new.append(prods)
                if not with_dots:
                    return 0
                return tuple(a + (p0 + p1) for a, p0, p1 in zip(acc, new[0], new[1]))
            init = (jnp.zeros((8, 384), F32),) * (KRYLOV_STEPS + 1) if with_dots else 0
            return lax.fori_loop(0, ROWS // 8, body, init)
        lax.fori_loop(0, NBLK, partner_wait, 0)
        acc = project(own0, True)
        for m in range(KRYLOV_STEPS + 1):
            put_row(K_SECOND, m, acc[m])
        sum_start(K_SECOND)
        project(oth0, False)
        total = sum_finish(K_SECOND)
        coef[1, 0:5] = total[0:5]
        scal[pl.ds(2, 1), :] = total[5:6, :]
        norm_scale()
        finalize(lax.rem(step + 1, KRYLOV_STEPS))
        return 0

    lax.fori_loop(0, KRYLOV_STEPS, krylov_step, 0)

    finish_norm(KRYLOV_STEPS)
    for copy in l_copies(0):
        copy.wait()

    def scale_out(i, _):
        row = pl.multiple_of(own0 + i * 16, 16)
        u[pl.ds(row, 16), :] = basis[0, pl.ds(row, 16), :] * scal[pl.ds(3, 1), :] * math.sqrt(4.0 * BOND * BOND)
        return 0
    lax.fori_loop(0, ROWS // 16, scale_out, 0)
    psi_out = pltpu.make_async_copy(u.at[pl.ds(own0, ROWS), :], out_psi, io_sem)
    psi_out.start()
    psi_out.wait()


def split3_xla(x):
    hi = lax.reduce_precision(x, 8, 7)
    rest = x - hi
    mid = lax.reduce_precision(rest, 8, 7)
    low = rest - mid
    return hi.astype(BF16), mid.astype(BF16), low.astype(BF16)


def mpo_matrix(w_mat):
    w0, w1, w2 = split3_xla(w_mat)
    zero = jnp.zeros_like(w0)
    return jnp.concatenate([jnp.concatenate([w0, w0, w0], axis=1),
                            jnp.concatenate([w1, w1, zero], axis=1),
                            jnp.concatenate([w2, zero, zero], axis=1)], axis=0)


def solution(mesh):
    psi_spec = P("left", None, None, "right")

    def local_fn(psi, env_left, env_right, mpo):
        odd = lax.rem(lax.axis_index("right"), 2) == 1
        psi4 = psi.reshape(ROWS, 4, COLS)
        main = jnp.where(odd, psi4[:, :, 64:], psi4[:, :, :128]).reshape(ROWS, 512)
        extra = jnp.where(odd, psi4[:, :, :64], psi4[:, :, 128:]).reshape(ROWS, 256)
        psi_q = jnp.concatenate([main, extra], axis=1)
        lefts = split3_xla(jnp.transpose(env_left, (1, 0, 2)))
        rights = split3_xla(jnp.transpose(env_right, (1, 0, 2)))
        w_rows = jnp.transpose(mpo.reshape(MPO, MPO, 4, 4), (1, 3, 2, 0)).reshape(80, 80)
        w_pairs = jnp.transpose(mpo.reshape(MPO, MPO, 2, 2, 4), (1, 4, 2, 0, 3)).reshape(80, 80)

        vmem = pl.BlockSpec(memory_space=pltpu.VMEM)
        hbm = pl.BlockSpec(memory_space=pl.ANY)
        dma = pltpu.SemaphoreType.DMA
        small, psi_new = pl.pallas_call(
            kernel,
            out_shape=(jax.ShapeDtypeStruct((16, 128), F32), jax.ShapeDtypeStruct((ROWS, BOND), F32)),
            in_specs=[hbm] * 7 + [vmem] * 2,
            out_specs=(vmem, hbm),
            scratch_shapes=[
                pltpu.VMEM((3, MPO, LB, BOND), BF16),
                pltpu.VMEM((3, MPO, 128, BOND), BF16),
                pltpu.VMEM((3, MPO, 64, BOND), BF16),
                pltpu.VMEM((3, BOND, BOND), BF16),
                pltpu.VMEM((80 * CS, 128), F32),
                pltpu.VMEM((80 * CX, 128), F32),
                pltpu.VMEM((80 * CS, 128), F32),
                pltpu.VMEM((80 * CX, 128), F32),
                pltpu.VMEM((3, 4 * LB, MPO * COLS), BF16),
                pltpu.VMEM((4 * LB, BOND), F32),
                pltpu.VMEM((2, N_RIGHT, LB, BOND), F32),
                pltpu.VMEM((N_RIGHT - 1, ROWS, BOND), F32),
                pltpu.VMEM((KRYLOV_STEPS, BOND, BOND), F32),
                pltpu.VMEM((BOND, BOND), F32),
                pltpu.VMEM((3, N_DEV, 8, 128), F32),
                pltpu.VMEM((2, 8, BOND), F32),
                pltpu.VMEM((8, BOND), F32),
                dma((3,)), dma((6,)), dma,
                dma((N_RIGHT - 1, 2)), dma((N_RIGHT - 1, NBLK)),
                dma((NBLK,)), dma((NBLK,)),
                dma((3, N_DEV - 1)), dma((3, N_DEV - 1)),
            ],
            compiler_params=pltpu.CompilerParams(
                collective_id=0, has_side_effects=True, vmem_limit_bytes=67_000_000),
            name="lanczos",
        )(psi_q, *lefts, *rights, mpo_matrix(w_rows), mpo_matrix(w_pairs))

        main = psi_new[:, :512].reshape(ROWS, 4, 128)
        extra = psi_new[:, 512:].reshape(ROWS, 4, 64)
        psi_next = jnp.where(odd, jnp.concatenate([extra, main], axis=2),
                             jnp.concatenate([main, extra], axis=2)).reshape(ROWS, 2, 2, COLS)
        return small[0:5, 0], small[9:14, 0], psi_next

    return jax.shard_map(
        local_fn,
        mesh=mesh,
        in_specs=(psi_spec, P("left", None, None), P("right", None, None), P()),
        out_specs=(P(), P(), psi_spec),
        check_vma=False,
    )
```

time: 1830 us -> 908 us (0.50)
  matrix products: 942 us -> 0 us
  Pallas kernels: 0 us -> 865 us
  blocking collectives: 374 us -> 0 us
  waiting for transfers between devices: 324 us -> 0 us
  local copies, waits for them, and re-layouts: 68.1 us -> 10.5 us
  other arithmetic: 87.5 us -> 32.3 us
    dot_general x15 -> x0, matrix products: 942 us -> none  [the longest x5 353 us: apply_ham(): jnp.einsum('rtvcb,bre->tvce', stage_two, env_right, precision=PREC_MODE,...]
    pallas_call x0 -> x1, Pallas kernels: none -> 865 us  [local_fn(): pl.pallas_call(kernel, out_shape=(jax.ShapeDtypeStruct((16, 128), F32), j...]
    psum x16 -> x0, blocking collectives: 374 us -> none  [the longest x10 232 us: global_dots(): return lax.psum(local_dots, BOTH_AXES)]
    reduce_scatter x5 -> x0, waiting for transfers between devices: 262 us -> none  [apply_ham(): lax.psum_scatter(part_out, 'right', scatter_dimension=3, tiled=True)]
    reduce_sum x16 -> x0, other arithmetic: 64.2 us -> none  [the longest x10 36.2 us: global_dots(): jnp.sum(basis_vec * residual)]
    all_gather x5 -> x0, waiting for transfers between devices: 41.1 us -> none  [apply_ham(): vec_full = lax.all_gather(in_vec, 'left', axis=0, tiled=True)]
    convert_element_type x0 -> x3, other arithmetic: none -> 26.6 us  [split3_xla(): return (hi.astype(BF16), mid.astype(BF16), low.astype(BF16))]
    all_to_all x1 -> x0, local copies, waits for them, and re-layouts: 25.8 us -> none  [local_fn(): left_full = lax.all_to_all(env_left, 'left', 2, 0, tiled=True)]
  transfers between devices with their start and end apart: 11 -> 0, of which waited for: 10 -> 0; matrix products, arithmetic and copies ran while one was open for 3% -> 0% of each run, Pallas kernels for 0% -> 0%
where the time goes in v1:
time: 908 us
  Pallas kernels  865 us (95%)
  other arithmetic  32.3 us (4%)
  local copies, waits for them, and re-layouts  10.5 us (1%)
    pallas_call x1, Pallas kernels, local_fn(): pl.pallas_call(kernel, out_shape=(jax.ShapeDtypeStruct((16, 128), F32), j...  865 us
    convert_element_type x3, other arithmetic, split3_xla(): return (hi.astype(BF16), mid.astype(BF16), low.astype(BF16))  26.6 us

profile of v1, /device:TPU:0, one launch (start us, length us, event | category | flops | bytes accessed | tf_op | source)
XLA Modules:
  0.0 908.1 jit_solution(11843832322415827991)
XLA Ops:
  0.6 0.0 copy-start.1
  0.6 1.2 copy.19
  1.8 0.1 reshape.42
  2.0 1.2 slice_select_fusion.1
  3.1 0.2 copy.18
  3.3 1.5 slice_select_fusion
  4.8 0.3 copy.26
  5.0 1.1 pad_maximum_fusion.psi
  6.1 0.0 copy-done.1
  6.1 0.6 copy.20
  6.7 0.3 reshape.44
  7.0 0.1 copy.21
  7.2 0.8 fusion.7
  8.0 0.0 copy-start
  8.0 13.6 %fusion.1 = (bf16[20,192,768]{2,1,0:T(8,128)(2,1)}, bf16[20,192,768]{2,1,0:T(8,128)(2,1)}, bf16[20,192,768]{2,1,0:T(8,128)(2,1)}) fusion(f32[192,20,768]{2,0,1:T(8,128)} %param.6), kind=kLoop, calls=%fused_computation.9 | loop fusion | flops 20643840 | bytes 29491200 | tf_op jit(solution)/shard_map/convert_element_type | solution.py:391
  21.6 3.8 copy-done
  25.4 13.0 %fusion = (bf16[20,384,768]{2,1,0:T(8,128)(2,1)}, bf16[20,384,768]{2,1,0:T(8,128)(2,1)}, bf16[20,384,768]{2,1,0:T(8,128)(2,1)}) fusion(f32[384,20,768]{2,0,1:T(8,128)S(1)} %copy-done), kind=kLoop, calls=%fused_computation.4 | loop fusion | flops 41287680 | bytes 58982400 | tf_op jit(solution)/shard_map/convert_element_type | solution.py:391
  38.3 864.6 %lanczos.1 = (f32[16,128]{1,0:T(8,128)}, f32[384,768]{1,0:T(8,128)}) custom-call(f32[384,768]{1,0:T(8,128)} %pad_maximum_fusion.psi, bf16[20,384,768]{2,1,0:T(8,128)(2,1)} %get-tuple-element.11.l_hi, bf16[20,384,768]{2,1,0:T(8,128)(2,1)} %get-tuple-element.10.l_mid, bf16[20,384,768]{2,1,0:T(8,128)(2,1)} %get-tuple-element.9.l_low, ...), custom_call_target="tpu_custom_call" | custom-call | tf_op jit(solution)/shard_map/lanczos/pallas_call | solution.py:419
  903.0 1.3 slice_reduce_fusion
  904.3 1.0 slice.30
  905.3 1.2 slice.31
  906.5 0.3 copy.27
  906.8 0.2 copy.23
  907.0 1.1 maximum_select_fusion
  (2 shorter events, 0.0 us)
Async XLA Ops:
  0.6 5.5 copy-start.1
  8.0 17.4 %copy-start = (f32[384,20,768]{2,0,1:T(8,128)S(1)}, f32[384,20,768]{2,0,1:T(8,128)}, u32[]{:S(2)}) copy-start(f32[384,20,768]{2,0,1:T(8,128)} %param.5) | copy-start | bytes 70778880

commit v2 on v1

--- a/solution.py
+++ b/solution.py
@@ -19,6 +19,7 @@
 NBLK = ROWS // LB
 HALF = LB // 2
 CS, CX = LB + 8, HALF + 8
+LC = 20
 UNITS = 16
 K_FIRST, K_SECOND, K_NORM = 0, 1, 2
 
@@ -165,7 +166,7 @@
                         out.append(acc[n] + (x2[:8] + x2[8:]))
                 return tuple(out) if with_norm else 0
             init = (jnp.zeros((8, 384), F32),) * 2 if with_norm else 0
-            return lax.fori_loop(0, ROWS // 16, body, init)
+            return lax.fori_loop(0, ROWS // 16, body, init, unroll=4)
         acc = rows(own0, True)
         put_row(K_NORM, 0, acc[0] + acc[1])
         rows(oth0, False)
@@ -198,13 +199,13 @@
     finalize(0)
 
     def stage_one(i, _):
-        l0 = i * 4
-        a = [lb[t, pl.ds(l0, 4)].reshape(4 * LB, BOND) for t in range(3)]
+        l0 = i * LC
+        a = [lb[t, pl.ds(l0, LC)].reshape(LC * LB, BOND) for t in range(3)]
         for n in range(3):
             t1 = dot6(a, [vs[t, :, n * 256:(n + 1) * 256] for t in range(3)])
             for h in range(2):
                 t1h = t1[:, h * 128:(h + 1) * 128]
-                for d in range(4):
+                for d in range(LC):
                     x = t1h[d * LB:(d + 1) * LB]
                     if n < 2:
                         row = pl.multiple_of(((2 * n + h) * MPO + l0 + d) * CS, 8)
@@ -287,20 +288,20 @@
         def block(blk, _):
             for copy in l_copies(blk):
                 copy.wait()
-            lax.fori_loop(0, MPO // 4, stage_one, 0)
+            lax.fori_loop(0, MPO // LC, stage_one, 0)
             for copy in l_copies(lax.rem(blk + 1, NBLK)):
                 copy.start()
             lax.fori_loop(0, LB // 2 // UNITS, mpo_units(t1m, zm, w_main, CS), 0)
             lax.fori_loop(0, HALF // 2 // UNITS, mpo_units(t1x, zx, w_extra, CX), 0)
-            lax.fori_loop(0, MPO, gather_main, 0)
-            lax.fori_loop(0, MPO // 2, gather_extra, 0)
+            lax.fori_loop(0, MPO, gather_main, 0, unroll=MPO)
+            lax.fori_loop(0, MPO // 2, gather_extra, 0, unroll=MPO // 2)
 
             @pl.when((step == 0) & (blk == 0))
             def _():
                 for copy in r_copies():
                     copy.wait()
 
-            lax.fori_loop(0, 3, stage_three, 0)
+            lax.fori_loop(0, 3, stage_three, 0, unroll=3)
             pack(blk)
             for copy in piece_copies(blk):
                 copy.start()
@@ -313,7 +314,7 @@
                     row = pl.multiple_of(i * 16, 16)
                     basis[step, pl.ds(row, 16), :] = basis[step, pl.ds(row, 16), :] * scal[pl.ds(3, 1), :]
                     return 0
-                lax.fori_loop(0, BOND // 16, rescale, 0)
+                lax.fori_loop(0, BOND // 16, rescale, 0, unroll=4)
 
             @pl.when(blk > 0)
             def _():
@@ -327,7 +328,7 @@
             row = pl.multiple_of(own0 + i * 8, 8)
             x = u[pl.ds(row, 8), :]
             return tuple(acc[m] + x * basis[m, pl.ds(row, 8), :] for m in range(KRYLOV_STEPS))
-        acc = lax.fori_loop(0, ROWS // 8, first, (jnp.zeros((8, BOND), F32),) * KRYLOV_STEPS)
+        acc = lax.fori_loop(0, ROWS // 8, first, (jnp.zeros((8, BOND), F32),) * KRYLOV_STEPS, unroll=4)
         for m in range(KRYLOV_STEPS):
             put_row(K_FIRST, m, acc[m])
         sum_start(K_FIRST)
@@ -353,7 +354,7 @@
                     return 0
                 return tuple(a + (p0 + p1) for a, p0, p1 in zip(acc, new[0], new[1]))
             init = (jnp.zeros((8, 384), F32),) * (KRYLOV_STEPS + 1) if with_dots else 0
-            return lax.fori_loop(0, ROWS // 8, body, init)
+            return lax.fori_loop(0, ROWS // 8, body, init, unroll=4)
         lax.fori_loop(0, NBLK, partner_wait, 0)
         acc = project(own0, True)
         for m in range(KRYLOV_STEPS + 1):

time: 908 us -> 835 us (0.920)
  Pallas kernels: 865 us -> 792 us
    pallas_call x1, Pallas kernels: 865 us -> 792 us  [local_fn(): pl.pallas_call(kernel, out_shape=(jax.ShapeDtypeStruct((16, 128), F32), j...]
where the time goes in v2:
time: 835 us
  Pallas kernels  792 us (95%)
  other arithmetic  32.3 us (4%)
  local copies, waits for them, and re-layouts  10.5 us (1%)
    pallas_call x1, Pallas kernels, local_fn(): pl.pallas_call(kernel, out_shape=(jax.ShapeDtypeStruct((16, 128), F32), j...  792 us
    convert_element_type x3, other arithmetic, split3_xla(): return (hi.astype(BF16), mid.astype(BF16), low.astype(BF16))  26.6 us

profile of v2, /device:TPU:0, one launch (start us, length us, event | category | flops | bytes accessed | tf_op | source)
XLA Modules:
  0.0 835.1 jit_solution(8653231991905835738)
XLA Ops:
  0.6 0.0 copy-start.1
  0.6 1.2 copy.19
  1.8 0.1 reshape.42
  2.0 1.2 slice_select_fusion.1
  3.1 0.2 copy.18
  3.3 1.5 slice_select_fusion
  4.8 0.3 copy.26
  5.0 1.1 pad_maximum_fusion.psi
  6.1 0.0 copy-done.1
  6.1 0.6 copy.20
  6.7 0.3 reshape.44
  7.0 0.1 copy.21
  7.2 0.8 fusion.7
  8.0 0.0 copy-start
  8.0 13.6 %fusion.1 = (bf16[20,192,768]{2,1,0:T(8,128)(2,1)}, bf16[20,192,768]{2,1,0:T(8,128)(2,1)}, bf16[20,192,768]{2,1,0:T(8,128)(2,1)}) fusion(f32[192,20,768]{2,0,1:T(8,128)} %param.6), kind=kLoop, calls=%fused_computation.9 | loop fusion | flops 20643840 | bytes 29491200 | tf_op jit(solution)/shard_map/convert_element_type | solution.py:392
  21.6 3.8 copy-done
  25.4 13.0 %fusion = (bf16[20,384,768]{2,1,0:T(8,128)(2,1)}, bf16[20,384,768]{2,1,0:T(8,128)(2,1)}, bf16[20,384,768]{2,1,0:T(8,128)(2,1)}) fusion(f32[384,20,768]{2,0,1:T(8,128)S(1)} %copy-done), kind=kLoop, calls=%fused_computation.4 | loop fusion | flops 41287680 | bytes 58982400 | tf_op jit(solution)/shard_map/convert_element_type | solution.py:392
  38.3 791.6 %lanczos.1 = (f32[16,128]{1,0:T(8,128)}, f32[384,768]{1,0:T(8,128)}) custom-call(f32[384,768]{1,0:T(8,128)} %pad_maximum_fusion.psi, bf16[20,384,768]{2,1,0:T(8,128)(2,1)} %get-tuple-element.11.l_hi, bf16[20,384,768]{2,1,0:T(8,128)(2,1)} %get-tuple-element.10.l_mid, bf16[20,384,768]{2,1,0:T(8,128)(2,1)} %get-tuple-element.9.l_low, ...), custom_call_target="tpu_custom_call" | custom-call | tf_op jit(solution)/shard_map/lanczos/pallas_call | solution.py:420
  830.0 1.3 slice_reduce_fusion
  831.3 1.0 slice.30
  832.4 1.2 slice.31
  833.5 0.3 copy.27
  833.8 0.2 copy.23
  834.0 1.1 maximum_select_fusion
  (2 shorter events, 0.0 us)
Async XLA Ops:
  0.6 5.5 copy-start.1
  8.0 17.4 %copy-start = (f32[384,20,768]{2,0,1:T(8,128)S(1)}, f32[384,20,768]{2,0,1:T(8,128)}, u32[]{:S(2)}) copy-start(f32[384,20,768]{2,0,1:T(8,128)} %param.5) | copy-start | bytes 70778880
